TPU v7x, 32 devices: a whole 2x2x4 slice. The times are simulated.
32 devices in a mesh: expert: 4 (over z), shard: 8 (over y, x, core).
Axes of the slice: x: 2, y: 2, z: 4, core: 2. Of those that a mesh axis runs over, the one named last changes fastest.
Arguments:
- master_gate: float32 [64, 2048, 1024], P('expert', 'shard'), may hold values from -0.1875 to 0.1875
- second_gate: float32 [64, 2048, 1024], P('expert', 'shard'), may hold values from -0.125 to 0.125
- master_up: float32 [64, 2048, 1024], P('expert', 'shard'), may hold values from -0.1875 to 0.1875
- second_up: float32 [64, 2048, 1024], P('expert', 'shard'), may hold values from -0.125 to 0.125
- mix_share: float32 [64], P('expert'), may hold values from 0.2 to 0.8
- router_weight: float32 [2048, 64], P('shard', 'expert'), may hold values from -0.125 to 0.125
- router_gain: float32 [2048], P('shard'), may hold values from 0.25 to 1.75
Outputs:
- final_gate: bfloat16 [64, 2048, 1024], P('expert', None, 'shard')
- final_up: bfloat16 [64, 2048, 1024], P('expert', None, 'shard')
- scale_gate: float32 [64, 1024], P('expert', 'shard')
- scale_up: float32 [64, 1024], P('expert', 'shard')
- serve_router: bfloat16 [2048, 64], replicated
All inputs are finite; a program needn't handle non-finite values.
Results may differ from a plain program's by a relative error of at most 0.001.
Values may be sent and summed in bfloat16 or wider, within the bound.
A program may use at most 256 MiB of HBM per device.

v0:
```python
import jax
import jax.numpy as jnp
from jax import lax
from jax.sharding import PartitionSpec as P

D_MODEL = 2048


def local(master_gate, second_gate, master_up, second_up, mix_share, router_weight, router_gain):
    merged_gate = (
        mix_share[:, None, None] * master_gate + (1.0 - mix_share[:, None, None]) * second_gate
    )
    merged_up = mix_share[:, None, None] * master_up + (1.0 - mix_share[:, None, None]) * second_up
    total_gate, total_up = lax.psum(
        (jnp.sum(jnp.abs(merged_gate), axis=1), jnp.sum(jnp.abs(merged_up), axis=1)), "shard"
    )
    scale_gate = total_gate / D_MODEL
    scale_up = total_up / D_MODEL
    narrow_gate, narrow_up = (
        (merged_gate / jnp.expand_dims(scale_gate, 1)).astype(jnp.bfloat16),
        (merged_up / jnp.expand_dims(scale_up, 1)).astype(jnp.bfloat16),
    )
    final_gate, final_up = (
        lax.all_to_all(narrow_gate, "shard", split_axis=2, concat_axis=1, tiled=True),
        lax.all_to_all(narrow_up, "shard", split_axis=2, concat_axis=1, tiled=True),
    )
    scale_gate = lax.dynamic_slice_in_dim(
        scale_gate, lax.axis_index("shard") * final_gate.shape[2], final_gate.shape[2], axis=1
    )
    scale_up = lax.dynamic_slice_in_dim(
        scale_up, lax.axis_index("shard") * final_up.shape[2], final_up.shape[2], axis=1
    )
    part_router = (router_weight * router_gain[:, None]).astype(jnp.bfloat16)
    row_router = lax.all_gather(part_router, "shard", axis=0, tiled=True)
    serve_router = lax.all_gather(row_router, "expert", axis=1, tiled=True)
    return (final_gate, final_up, scale_gate, scale_up, serve_router)


def solution(mesh):
    placed = (
        P("expert", "shard", None),
        P("expert", "shard", None),
        P("expert", "shard", None),
        P("expert", "shard", None),
        P("expert"),
        P("shard", "expert"),
        P("shard"),
    )
    return jax.shard_map(
        local,
        mesh=mesh,
        in_specs=placed,
        out_specs=(
            P("expert", None, "shard"),
            P("expert", None, "shard"),
            P("expert", "shard"),
            P("expert", "shard"),
            P(),
        ),
        check_vma=False,
    )
```

profile of v0, /device:TPU:0, one launch (start us, length us, event | category | flops | bytes accessed | tf_op | source)
XLA Modules:
  0.0 434.8 jit_solution(18230987575285412976)
XLA Ops:
  7.2 0.0 all-reduce.3.cloned.1.call-start
  7.2 17.6 %copy.22 = f32[16,256,1024]{1,0,2:T(8,128)} copy(f32[16,256,1024]{2,1,0:T(8,128)} %param.7) | data formatting | bytes 33554432 | tf_op args[0]
  24.8 17.6 %copy.23 = f32[16,256,1024]{1,0,2:T(8,128)} copy(f32[16,256,1024]{2,1,0:T(8,128)} %param.8) | data formatting | bytes 33554432 | tf_op args[1]
  42.4 17.6 %copy.25 = f32[16,256,1024]{1,0,2:T(8,128)} copy(f32[16,256,1024]{2,1,0:T(8,128)} %param.9) | data formatting | bytes 33554432 | tf_op args[2]
  60.0 0.0 copy-start.1
  60.0 17.6 %copy.26 = f32[16,256,1024]{1,0,2:T(8,128)} copy(f32[16,256,1024]{2,1,0:T(8,128)} %param.10) | data formatting | bytes 33554432 | tf_op args[3]
  77.6 0.0 copy-done.1
  77.6 23.7 %abs_reduce_fusion = (f32[16,1024]{0,1:T(8,128)}, f32[16,1024]{0,1:T(8,128)}) fusion(f32[16,256,1024]{1,0,2:T(8,128)} %copy.26, f32[16]{0:T(128)S(1)} %broadcast_subtract_fusion, f32[16,256,1024]{1,0,2:T(8,128)} %copy.25, f32[16]{0:T(128)S(1)} %copy-done.1, f32[16,256,1024]{1,0,2:T(8,128)} %copy.23, f32[16,256,1024]{1,0,2:T(8,128)} %copy.22), kind=kLoop, calls=%fused_computation.1 | loop fusion | flops 41910272 | bytes 67240064 | tf_op jit(solution)/shard_map/reduce_sum | solution.py:15
  101.3 0.0 all-reduce.3.cloned.1.call-update
  101.4 59.6 %all-reduce.3.cloned.1.call-done = (f32[16,1024]{0,1:T(8,128)}, f32[16,1024]{0,1:T(8,128)}) async-done(((f32[16,1024]{0,1:T(8,128)}, f32[16,1024]{0,1:T(8,128)}), (f32[16,1024]{0,1:T(8,128)}, f32[16,1024]{0,1:T(8,128)})) %all-reduce.3.cloned.1.call-update) | async-done | bytes 131088 | tf_op jit(solution)/shard_map/psum | solution.py:14
  161.0 1.3 broadcast_multiply_fusion
  162.3 25.3 %divide_convert_fusion = (bf16[16,256,1024]{1,0,2:T(8,128)(2,1)}, bf16[16,256,1024]{1,0,2:T(8,128)(2,1)S(1)}) fusion(f32[16,1024]{0,1:T(8,128)S(1)} %get-tuple-element.16, f32[16,256,1024]{1,0,2:T(8,128)} %copy.26, f32[16]{0:T(128)S(1)} %broadcast_subtract_fusion, f32[16,256,1024]{1,0,2:T(8,128)} %copy.25, f32[16]{0:T(128)S(1)} %copy-done.1, ...), kind=kLoop, calls=%fused_computation | loop fusion | flops 41943040 | bytes 84017280 | tf_op jit(solution)/shard_map/convert_element_type | solution.py:21
  187.6 0.0 copy-start
  187.6 0.0 copy-start.2
  187.6 97.6 %all_to_all.36 = bf16[16,256,1024]{1,0,2:T(8,128)(2,1)} all-to-all(bf16[16,256,1024]{1,0,2:T(8,128)(2,1)S(1)} %get-tuple-element.15), channel_id=1, replica_groups=mesh['expert'=4,'shard'=8] {'shard'}, dimensions={2} | all-to-all | bytes 16777216 | tf_op jit(solution)/shard_map/all_to_all | solution.py:24
  285.2 4.9 %all-to-all-start.1 = ((bf16[16,256,1024]{1,0,2:T(8,128)(2,1)}), bf16[16,256,1024]{1,0,2:T(8,128)(2,1)}, u32[]{:S(2)}, u32[]{:S(2)}) async-start(bf16[16,256,1024]{1,0,2:T(8,128)(2,1)} %get-tuple-element.14), calls=%async_computation.1 | async-start | bytes 16777216 | tf_op jit(solution)/shard_map/all_to_all | solution.py:25
  290.2 0.0 copy-done
  290.2 0.0 copy-done.2
  290.2 97.2 %all_gather.6 = bf16[2048,16]{0,1:T(8,128)(2,1)S(1)} all-gather(bf16[256,16]{0,1:T(8,128)(2,1)S(1)} %multiply_convert_fusion), channel_id=1, replica_groups=mesh['expert'=4,'shard'=8] {'shard'}, dimensions={0}, use_global_device_ids=true | all-gather | bytes 73728 | tf_op jit(solution)/shard_map/all_gather | solution.py:34
  387.4 14.0 %all_gather.7 = bf16[2048,64]{0,1:T(8,128)(2,1)S(1)} all-gather(bf16[2048,16]{0,1:T(8,128)(2,1)S(1)} %all_gather.6), channel_id=1, replica_groups=mesh['expert'=4,'shard'=8] {'expert'}, dimensions={1}, use_global_device_ids=true | all-gather | bytes 327680 | tf_op jit(solution)/shard_map/all_gather | solution.py:35
  401.3 0.7 copy.28
  402.0 0.7 copy.29
  402.7 12.3 %copy.24 = bf16[16,8,256,128]{3,2,1,0:T(8,128)(2,1)} copy(bf16[16,8,256,128]{2,0,3,1:T(8,128)(2,1)} %bitcast.8) | data formatting | bytes 16777216 | tf_op jit(solution)/shard_map/all_to_all | solution.py:24
  415.0 0.0 all-to-all-done.1
  415.0 12.3 %copy.27 = bf16[16,8,256,128]{3,2,1,0:T(8,128)(2,1)} copy(bf16[16,8,256,128]{2,0,3,1:T(8,128)(2,1)} %bitcast.4) | data formatting | bytes 16777216 | tf_op jit(solution)/shard_map/all_to_all | solution.py:25
  427.2 0.7 copy.33
  (4 shorter events, 0.0 us)
Async XLA Ops:
  7.2 153.8 %all-reduce.3.cloned.1.call-start = ((), (), s32[]{:S(2)}) async-start(), calls=%async_computation.2 | async-start | bytes 2097152 | tf_op jit(solution)/shard_map/psum | solution.py:14
  60.0 17.6 %copy-start.1 = (f32[16]{0:T(128)S(1)}, f32[16]{0:T(128)}, u32[]{:S(2)}) copy-start(f32[16]{0:T(128)} %param.11) | copy-start | bytes 196
  187.6 102.6 %copy-start = (f32[256,16]{0,1:T(8,128)S(1)}, f32[256,16]{0,1:T(8,128)}, u32[]{:S(2)}) copy-start(f32[256,16]{0,1:T(8,128)} %param.12) | copy-start | bytes 49156
  187.6 102.6 %copy-start.2 = (f32[256]{0:T(256)S(1)}, f32[256]{0:T(256)}, u32[]{:S(2)}) copy-start(f32[256]{0:T(256)} %param.13) | copy-start | bytes 3076
  285.2 129.8 %all-to-all-start.1 = ((bf16[16,256,1024]{1,0,2:T(8,128)(2,1)}), bf16[16,256,1024]{1,0,2:T(8,128)(2,1)}, u32[]{:S(2)}, u32[]{:S(2)}) async-start(bf16[16,256,1024]{1,0,2:T(8,128)(2,1)} %get-tuple-element.14), calls=%async_computation.1 | async-start | bytes 16777216 | tf_op jit(solution)/shard_map/all_to_all | solution.py:25
Sparse Core Ops, SparseCore 0:
  101.5 59.4 all-reduce.2
where the time goes:
time: 437 us; the launch traced here: 435 us
  blocking collectives  209 us (48%)
  local copies, waits for them, and re-layouts  97 us (22%)
  waiting for transfers between devices  59.7 us (14%)
  other arithmetic  50.3 us (12%)
  between operations  14.1 us (3%)
  starting transfers between devices  4.98 us (1%)
    all_to_all x1, blocking collectives, local(): lax.all_to_all(narrow_gate, 'shard', split_axis=2, concat_axis=1, tiled=T...  97.6 us
    all_gather x1, blocking collectives, local(): row_router = lax.all_gather(part_router, 'shard', axis=0, tiled=True)  97.2 us
    unnamed x13, local copies, waits for them, and re-layouts  72.5 us
    psum x1, waiting for transfers between devices, local(): lax.psum((jnp.sum(jnp.abs(merged_gate), axis=1), jnp.sum(jnp.abs(merged_u...  59.6 us
    convert_element_type x1, other arithmetic, local(): (merged_up / jnp.expand_dims(scale_up, 1)).astype(jnp.bfloat16)  25.3 us
    reduce_sum x1, other arithmetic, local(): jnp.sum(jnp.abs(merged_up), axis=1)  23.7 us
    all_gather x1, blocking collectives, local(): serve_router = lax.all_gather(row_router, 'expert', axis=1, tiled=True)  14 us
    all_to_all x1, local copies, waits for them, and re-layouts, local(): lax.all_to_all(narrow_up, 'shard', split_axis=2, concat_axis=1, tiled=True)  12.3 us
  transfers between devices with their start and end apart: 2, of which 1 were waited for; matrix products, arithmetic and copies ran while one was open for 3% of the time, Pallas kernels for 0%

commit v1 on v0

--- a/solution.py
+++ b/solution.py
@@ -31,7 +31,14 @@
         scale_up, lax.axis_index("shard") * final_up.shape[2], final_up.shape[2], axis=1
     )
     part_router = (router_weight * router_gain[:, None]).astype(jnp.bfloat16)
-    row_router = lax.all_gather(part_router, "shard", axis=0, tiled=True)
+    ring = [part_router]
+    for hop in range(7):
+        ring.append(lax.ppermute(ring[-1], "shard", [(dev, (dev + 1) % 8) for dev in range(8)]))
+    row_router = jnp.roll(
+        jnp.concatenate(ring[::-1], axis=0),
+        (lax.axis_index("shard") + 1) * ring[0].shape[0],
+        axis=0,
+    )
     serve_router = lax.all_gather(row_router, "expert", axis=1, tiled=True)
     return (final_gate, final_up, scale_gate, scale_up, serve_router)
 

time: 437 us -> 457 us (1.046)
  waiting for transfers between devices: 59.7 us -> 177 us
  blocking collectives: 209 us -> 112 us
    ppermute x0 -> x7, waiting for transfers between devices: none -> 117 us  [local(): lax.ppermute(ring[-1], 'shard', [(dev, (dev + 1) % 8) for dev in range(8)])]
    all_gather x1 -> x0, blocking collectives: 97.2 us -> none  [local(): row_router = lax.all_gather(part_router, 'shard', axis=0, tiled=True)]
    unnamed x13 -> x27, local copies, waits for them, and re-layouts: 72.5 us -> 72.5 us
  transfers between devices with their start and end apart: 2 -> 9, of which waited for: 1 -> 8; matrix products, arithmetic and copies ran while one was open for 3% -> 3% of each run, Pallas kernels for 0% -> 0%
where the time goes in v1:
time: 457 us; the launch traced here: 456 us
  waiting for transfers between devices  177 us (39%)
  blocking collectives  112 us (25%)
  local copies, waits for them, and re-layouts  97 us (21%)
  other arithmetic  50.3 us (11%)
  between operations  14.2 us (3%)
  starting transfers between devices  5.42 us (1%)
    ppermute x7, waiting for transfers between devices, local(): lax.ppermute(ring[-1], 'shard', [(dev, (dev + 1) % 8) for dev in range(8)])  117 us
    all_to_all x1, blocking collectives, local(): lax.all_to_all(narrow_gate, 'shard', split_axis=2, concat_axis=1, tiled=T...  97.6 us
    unnamed x27, local copies, waits for them, and re-layouts  72.5 us
    psum x1, waiting for transfers between devices, local(): lax.psum((jnp.sum(jnp.abs(merged_gate), axis=1), jnp.sum(jnp.abs(merged_u...  59.6 us
    convert_element_type x1, other arithmetic, local(): (merged_up / jnp.expand_dims(scale_up, 1)).astype(jnp.bfloat16)  25.3 us
    reduce_sum x1, other arithmetic, local(): jnp.sum(jnp.abs(merged_up), axis=1)  23.7 us
    all_gather x1, blocking collectives, local(): serve_router = lax.all_gather(row_router, 'expert', axis=1, tiled=True)  14.3 us
    all_to_all x1, local copies, waits for them, and re-layouts, local(): lax.all_to_all(narrow_up, 'shard', split_axis=2, concat_axis=1, tiled=True)  12.3 us
  transfers between devices with their start and end apart: 9, of which 8 were waited for; matrix products, arithmetic and copies ran while one was open for 3% of the time, Pallas kernels for 0%

profile of v1, /device:TPU:0, one launch (start us, length us, event | category | flops | bytes accessed | tf_op | source)
XLA Modules:
  0.0 455.5 jit_solution(7200855650547834946)
XLA Ops:
  7.2 0.0 all-reduce.3.cloned.1.call-start
  7.2 17.6 %copy.26 = f32[16,256,1024]{1,0,2:T(8,128)} copy(f32[16,256,1024]{2,1,0:T(8,128)} %param.10) | data formatting | bytes 33554432 | tf_op args[3]
  24.8 17.6 %copy.25 = f32[16,256,1024]{1,0,2:T(8,128)} copy(f32[16,256,1024]{2,1,0:T(8,128)} %param.9) | data formatting | bytes 33554432 | tf_op args[2]
  42.5 17.6 %copy.23 = f32[16,256,1024]{1,0,2:T(8,128)} copy(f32[16,256,1024]{2,1,0:T(8,128)} %param.8) | data formatting | bytes 33554432 | tf_op args[1]
  60.0 17.6 %copy.22 = f32[16,256,1024]{1,0,2:T(8,128)} copy(f32[16,256,1024]{2,1,0:T(8,128)} %param.7) | data formatting | bytes 33554432 | tf_op args[0]
  77.6 23.7 %abs_reduce_fusion = (f32[16,1024]{0,1:T(8,128)}, f32[16,1024]{0,1:T(8,128)}) fusion(f32[16,256,1024]{1,0,2:T(8,128)} %copy.26, f32[16]{0:T(128)S(1)} %broadcast_subtract_fusion, f32[16,256,1024]{1,0,2:T(8,128)} %copy.25, f32[16]{0:T(128)S(1)} %copy-done.2, f32[16,256,1024]{1,0,2:T(8,128)} %copy.23, f32[16,256,1024]{1,0,2:T(8,128)} %copy.22), kind=kLoop, calls=%fused_computation.1 | loop fusion | flops 41910272 | bytes 67240064 | tf_op jit(solution)/shard_map/reduce_sum | solution.py:15
  101.3 0.0 all-reduce.3.cloned.1.call-update
  101.3 59.6 %all-reduce.3.cloned.1.call-done = (f32[16,1024]{0,1:T(8,128)}, f32[16,1024]{0,1:T(8,128)}) async-done(((f32[16,1024]{0,1:T(8,128)}, f32[16,1024]{0,1:T(8,128)}), (f32[16,1024]{0,1:T(8,128)}, f32[16,1024]{0,1:T(8,128)})) %all-reduce.3.cloned.1.call-update) | async-done | bytes 131088 | tf_op jit(solution)/shard_map/psum | solution.py:14
  161.0 1.3 broadcast_multiply_fusion
  162.3 25.3 %divide_convert_fusion = (bf16[16,256,1024]{1,0,2:T(8,128)(2,1)}, bf16[16,256,1024]{1,0,2:T(8,128)(2,1)S(1)}) fusion(f32[16,1024]{0,1:T(8,128)S(1)} %get-tuple-element.16, f32[16,256,1024]{1,0,2:T(8,128)} %copy.26, f32[16]{0:T(128)S(1)} %broadcast_subtract_fusion, f32[16,256,1024]{1,0,2:T(8,128)} %copy.25, f32[16]{0:T(128)S(1)} %copy-done.2, ...), kind=kLoop, calls=%fused_computation | loop fusion | flops 41943040 | bytes 84017280 | tf_op jit(solution)/shard_map/convert_element_type | solution.py:21
  187.6 97.6 %all_to_all.36 = bf16[16,256,1024]{1,0,2:T(8,128)(2,1)} all-to-all(bf16[16,256,1024]{1,0,2:T(8,128)(2,1)S(1)} %get-tuple-element.15), channel_id=1, replica_groups=mesh['expert'=4,'shard'=8] {'shard'}, dimensions={2} | all-to-all | bytes 16777216 | tf_op jit(solution)/shard_map/all_to_all | solution.py:24
  285.2 4.9 %all-to-all-start.1 = ((bf16[16,256,1024]{1,0,2:T(8,128)(2,1)}), bf16[16,256,1024]{1,0,2:T(8,128)(2,1)}, u32[]{:S(2)}, u32[]{:S(2)}) async-start(bf16[16,256,1024]{1,0,2:T(8,128)(2,1)} %get-tuple-element.14), calls=%async_computation.1 | async-start | bytes 16777216 | tf_op jit(solution)/shard_map/all_to_all | solution.py:25
  290.2 0.4 collective-permute-start
  290.6 93.1 %collective-permute-done = bf16[256,16]{0,1:T(8,128)(2,1)S(1)} collective-permute-done((bf16[256,16]{0,1:T(8,128)(2,1)S(1)}, bf16[256,16]{0,1:T(8,128)(2,1)S(1)}, u32[]{:S(2)}, u32[]{:S(2)}) %collective-permute-start) | collective-permute-done | bytes 8224 | tf_op jit(solution)/shard_map/ppermute | solution.py:36
  383.7 0.0 collective-permute-start.1
  383.7 4.0 collective-permute-done.1
  387.7 0.0 collective-permute-start.2
  387.7 4.0 collective-permute-done.2
  391.6 4.0 collective-permute-done.3
  395.6 0.0 collective-permute-start.4
  395.6 4.0 collective-permute-done.4
  399.6 0.0 collective-permute-start.5
  399.6 4.0 collective-permute-done.5
  403.6 0.0 collective-permute-start.6
  403.6 4.0 collective-permute-done.6
  407.7 14.3 %all_gather.3 = bf16[2048,64]{0,1:T(8,128)(2,1)S(1)} all-gather(bf16[2048,16]{0,1:T(8,128)(2,1)S(1)} %constant_dynamic-slice_fusion), channel_id=1, replica_groups=mesh['expert'=4,'shard'=8] {'expert'}, dimensions={1}, use_global_device_ids=true | all-gather | bytes 327680 | tf_op jit(solution)/shard_map/all_gather | solution.py:42
  422.1 0.7 copy.28
  422.7 0.7 copy.29
  423.4 12.3 %copy.24 = bf16[16,8,256,128]{3,2,1,0:T(8,128)(2,1)} copy(bf16[16,8,256,128]{2,0,3,1:T(8,128)(2,1)} %bitcast.8) | data formatting | bytes 16777216 | tf_op jit(solution)/shard_map/all_to_all | solution.py:24
  435.7 0.0 all-to-all-done.1
  435.7 12.3 %copy.27 = bf16[16,8,256,128]{3,2,1,0:T(8,128)(2,1)} copy(bf16[16,8,256,128]{2,0,3,1:T(8,128)(2,1)} %bitcast.4) | data formatting | bytes 16777216 | tf_op jit(solution)/shard_map/all_to_all | solution.py:25
  448.0 0.7 copy.48
  (28 shorter events, 0.1 us)
Async XLA Ops:
  7.2 17.7 %copy-start.2 = (f32[16]{0:T(128)S(1)}, f32[16]{0:T(128)}, u32[]{:S(2)}) copy-start(f32[16]{0:T(128)} %param.11) | copy-start | bytes 196
  7.2 153.8 %all-reduce.3.cloned.1.call-start = ((), (), s32[]{:S(2)}) async-start(), calls=%async_computation.2 | async-start | bytes 2097152 | tf_op jit(solution)/shard_map/psum | solution.py:14
  187.6 102.6 %copy-start = (f32[256,16]{0,1:T(8,128)S(1)}, f32[256,16]{0,1:T(8,128)}, u32[]{:S(2)}) copy-start(f32[256,16]{0,1:T(8,128)} %param.12) | copy-start | bytes 49156
  187.6 102.6 %copy-start.1 = (f32[256]{0:T(256)S(1)}, f32[256]{0:T(256)}, u32[]{:S(2)}) copy-start(f32[256]{0:T(256)} %param.13) | copy-start | bytes 3076
  285.2 150.5 %all-to-all-start.1 = ((bf16[16,256,1024]{1,0,2:T(8,128)(2,1)}), bf16[16,256,1024]{1,0,2:T(8,128)(2,1)}, u32[]{:S(2)}, u32[]{:S(2)}) async-start(bf16[16,256,1024]{1,0,2:T(8,128)(2,1)} %get-tuple-element.14), calls=%async_computation.1 | async-start | bytes 16777216 | tf_op jit(solution)/shard_map/all_to_all | solution.py:25
  290.2 93.5 %collective-permute-start = (bf16[256,16]{0,1:T(8,128)(2,1)S(1)}, bf16[256,16]{0,1:T(8,128)(2,1)S(1)}, u32[]{:S(2)}, u32[]{:S(2)}) collective-permute-start(bf16[256,16]{0,1:T(8,128)(2,1)S(1)} %multiply_convert_fusion), channel_id=1, source_target_pairs={{0,1},{1,2},{2,3},{3,4},{4,5},{5,6},{6,7},{7,0},{8,9},{9,10},{10,1... | collective-permute-start | bytes 24584 | tf_op jit(solution)/shard_map/ppermute | solution.py:36
  383.7 4.0 collective-permute-start.1
  387.7 4.0 collective-permute-start.2
  391.6 4.0 collective-permute-start.3
  395.6 4.0 collective-permute-start.4
  399.6 4.0 collective-permute-start.5
  403.6 4.0 collective-permute-start.6
Sparse Core Ops, SparseCore 0:
  101.5 59.4 all-reduce.2
